TPU v7x, 32 devices: a whole 2x2x4 slice. The times are simulated.
32 devices in a mesh: gx: 4 (over y, x), gy: 4 (over z), gz: 2 (over core).
Axes of the slice: x: 2, y: 2, z: 4, core: 2. Of those that a mesh axis runs over, the one named last changes fastest.
Arguments:
- fields: bfloat16 [4096, 2048], P(('gx', 'gy', 'gz')), may hold values from -6 to 6
- coordinates: float32 [3, 524288], P(None, ('gx', 'gy', 'gz')), may hold values from -1 to 1
- element_rank: int32 [524288, 1], P(('gx', 'gy', 'gz')), may hold values from 0 to 31; in each aligned block of 16384 rows (0 to 16383, 16384 to 32767, ...) at most 640 rows name the same one
- element_slot: int32 [524288], P(('gx', 'gy', 'gz')), may hold values from 0 to 127
Outputs:
- samples: float32 [4, 524288], P(None, ('gx', 'gy', 'gz'))
Inputs may be any that keep to these rules, and one draw needn't show every extreme that they name: `element_rank`: among the probes of one device no rank is named by more than 640 probes, and in some devices' blocks one rank is named by exactly 640.
All inputs are finite; a program needn't handle non-finite values.
Results may differ from a plain program's by a relative error of at most 0.0024.
Values sent between devices are 32-bit elements; how exact they have to be, the bound alone decides.
A program may use at most 64 MiB of HBM per device.

v0:
```python
import math

import jax
import jax.numpy as jnp
import numpy as np
from jax import lax
from jax.sharding import PartitionSpec as P

gll_points = np.array(
    [
        -1.0,
        -0.8717401485096066,
        -0.5917001814331423,
        -0.2092992179024789,
        0.2092992179024789,
        0.5917001814331423,
        0.8717401485096066,
        1.0,
    ]
)
gll_scale = np.array(
    [1.0 / np.prod([gll_points[a] - gll_points[b] for b in range(8) if b != a]) for a in range(8)]
)


def lagrange(coord):
    offsets = coord[None, :] - jnp.asarray(gll_points, coord.dtype)[:, None]
    weights = []
    for node_a in range(8):
        factor = jnp.ones_like(coord) * gll_scale[node_a]
        for node_b in range(8):
            if node_b != node_a:
                factor = factor * offsets[node_b]
        weights.append(factor)
    return jnp.stack(weights, axis=0)


def interpolate(payload, fields):
    total_rows = payload.shape[1]
    local_count = fields.shape[0]
    block_rows = math.gcd(total_rows, 2048)
    block_count = total_rows // block_rows
    element_ids = jnp.arange(local_count, dtype=jnp.int32)

    def one_block(block):
        weight_r = lagrange(block[0])
        weight_s = lagrange(block[1])
        weight_t = lagrange(block[2]).astype(jnp.bfloat16)
        slots_block = block[3].astype(jnp.int32)
        picker = (slots_block[:, None] == element_ids[None, :]).astype(jnp.bfloat16)
        gathered = jnp.dot(picker, fields, preferred_element_type=jnp.float32).astype(jnp.bfloat16)
        gathered = gathered.reshape(block_rows, 256, 8)
        along_t = jnp.einsum("nak,kn->na", gathered, weight_t, preferred_element_type=jnp.float32)
        along_t = along_t.reshape(block_rows, 4, 8, 8)
        along_s = jnp.einsum("nfij,jn->nfi", along_t, weight_s, precision=lax.Precision.HIGHEST)
        return jnp.einsum("nfi,in->fn", along_s, weight_r, precision=lax.Precision.HIGHEST)

    blocks = payload.reshape(4, block_count, block_rows).transpose(1, 0, 2)
    result = lax.map(one_block, blocks)
    return result.transpose(1, 0, 2).reshape(4, total_rows)


def local(fields, coordinates, element_rank, element_slot):
    devices = lax.axis_size(("gx", "gy", "gz"))
    probes = element_slot.shape[0]
    capacity = 5 * probes // (4 * devices)
    target = element_rank[:, 0]
    group_rows = math.gcd(probes, 512)
    group_count = probes // group_rows
    onehot = (target[:, None] == jnp.arange(devices, dtype=jnp.int32)[None, :]).astype(jnp.bfloat16)
    onehot = onehot.reshape(group_count, group_rows, devices)
    lower = jnp.arange(group_rows)
    triangle = (lower[:, None] >= lower[None, :]).astype(jnp.bfloat16)
    within = jnp.einsum("ij,bjd->bid", triangle, onehot, preferred_element_type=jnp.float32)
    totals = within[:, -1, :]
    offsets = jnp.cumsum(totals, axis=0) - totals
    counted = (within + offsets[:, None, :]) * onehot.astype(jnp.float32)
    position = (jnp.sum(counted, axis=2).reshape(probes) - 1.0).astype(jnp.int32)
    flat = target * capacity + position
    payload = jnp.concatenate([coordinates, element_slot.astype(jnp.float32)[None, :]], axis=0)
    send = jnp.zeros((4, devices * capacity), jnp.float32).at[:, flat].set(payload)
    arrived = lax.all_to_all(
        send.reshape(4, devices, capacity),
        ("gx", "gy", "gz"),
        split_axis=1,
        concat_axis=1,
        tiled=True,
    )
    width = arrived.shape[2]
    values = interpolate(arrived.reshape(4, -1), fields)
    values = values.reshape(4, devices, width)
    returned = lax.all_to_all(values, ("gx", "gy", "gz"), split_axis=1, concat_axis=1, tiled=True)
    return returned.reshape(4, devices * capacity)[:, flat]


def solution(mesh):
    placed = (
        P(("gx", "gy", "gz"), None),
        P(None, ("gx", "gy", "gz")),
        P(("gx", "gy", "gz"), None),
        P(("gx", "gy", "gz")),
    )
    return jax.shard_map(
        local, mesh=mesh, in_specs=placed, out_specs=P(None, ("gx", "gy", "gz")), check_vma=False
    )
```

profile of v0, /device:TPU:0, one launch (start us, length us, event | category | flops | bytes accessed | tf_op | source)
XLA Modules:
  0.0 265.9 jit_solution(6529468678508932925)
XLA Ops:
  0.0 0.5 broadcast.166
  0.5 1.6 reduce.11
  2.2 0.8 fusion.8
  3.1 0.3 copy.30
  3.4 0.3 copy.31
  3.7 0.4 subtract_reduce_fusion
  4.1 0.6 multiply_reduce_fusion.3
  5.1 5.1 %copy.32 = f32[16384,4]{1,0:T(8,128)} copy(f32[16384,4]{0,1:T(4,128)S(1)} %maximum_bitcast_fusion) | data formatting | bytes 524288 | tf_op jit(solution)/shard_map/concatenate | solution.py:80
  10.2 45.3 %scatter_custom_fusion = f32[4,20480]{0,1:T(8,128)} fusion(s32[16384]{0:T(1024)S(1)} %bitcast.89, f32[16384,4]{1,0:T(8,128)} %copy.32, f32[]{:T(128)} %constant.13.clone.1), kind=kCustom, calls=%fused_computation.42 | custom fusion | bytes 328192 | tf_op jit(solution)/shard_map/scatter | solution.py:81
  55.6 6.7 %copy.33 = f32[4,32,640]{2,0,1:T(4,128)} copy(f32[4,32,640]{0,2,1:T(8,128)} %bitcast.80) | data formatting | bytes 655360 | tf_op jit(solution)/shard_map/reshape | solution.py:83
  62.2 7.5 %all-to-all-start = ((f32[4,32,640]{2,0,1:T(4,128)}), f32[4,32,640]{2,0,1:T(4,128)S(1)}, u32[]{:S(2)}, u32[]{:S(2)}) async-start(f32[4,32,640]{2,0,1:T(4,128)} %copy.33), calls=%async_computation | async-start | bytes 655360 | tf_op jit(solution)/shard_map/all_to_all | solution.py:82
  69.8 11.8 %all-to-all-done = f32[4,32,640]{2,0,1:T(4,128)S(1)} async-done(((f32[4,32,640]{2,0,1:T(4,128)}), f32[4,32,640]{2,0,1:T(4,128)S(1)}, u32[]{:S(2)}, u32[]{:S(2)}) %all-to-all-start) | async-done | bytes 327712 | tf_op jit(solution)/shard_map/all_to_all | solution.py:82
  81.7 99.4 %while.13 = (s32[]{:T(128)}, f32[10,4,2048]{2,1,0:T(4,128)}, f32[10,4,2048]{2,0,1:T(8,128)S(1)}, bf16[128,2048]{1,0:T(8,128)(2,1)}, s32[]{:T(128)}, /*index=5*/f32[8]{0:T(128)S(1)}, s32[]{:T(128)}, s32[]{}, s32[]{}, s32[]{}) while((s32[]{:T(128)}, f32[10,4,2048]{2,1,0:T(4,128)}, ...), condition=%wide.region_4.5_spmd.clone.clone.clone, body=%wide.region_3.4_spmd.sunk.clone.clone.clone.sunk | while | flops 1091790848 | bytes 7209657 | solution.py:59
  82.3 7.2 %multiply_reduce_fusion.7 = f32[2048,256]{0,1:T(8,128)S(1)} fusion(f32[2048,8]{0,1:T(8,128)S(1)} %bitcast_convert_fusion.2, bf16[128,2048]{1,0:T(8,128)(2,1)} %get-tuple-element.256, s32[2048]{0:T(1024)S(1)} %bitcast.93), kind=kOutput, calls=%fused_computation.3.clone.1 | convolution fusion | flops 1090256896 | bytes 2695168 | tf_op jit(solution)/shard_map/while/body/eval_jaxpr/dot_general | solution.py:51
  89.9 0.7 multiply_reduce_fusion.8
  91.1 0.6 bitcast_dynamic-update-slice_fusion.2
  92.2 7.2 %multiply_reduce_fusion.7 = f32[2048,256]{0,1:T(8,128)S(1)} fusion(f32[2048,8]{0,1:T(8,128)S(1)} %bitcast_convert_fusion.2, bf16[128,2048]{1,0:T(8,128)(2,1)} %get-tuple-element.256, s32[2048]{0:T(1024)S(1)} %bitcast.93), kind=kOutput, calls=%fused_computation.3.clone.1 | convolution fusion | flops 1090256896 | bytes 2695168 | tf_op jit(solution)/shard_map/while/body/eval_jaxpr/dot_general | solution.py:51
  99.8 0.7 multiply_reduce_fusion.8
  101.0 0.6 bitcast_dynamic-update-slice_fusion.2
  102.2 7.2 %multiply_reduce_fusion.7 = f32[2048,256]{0,1:T(8,128)S(1)} fusion(f32[2048,8]{0,1:T(8,128)S(1)} %bitcast_convert_fusion.2, bf16[128,2048]{1,0:T(8,128)(2,1)} %get-tuple-element.256, s32[2048]{0:T(1024)S(1)} %bitcast.93), kind=kOutput, calls=%fused_computation.3.clone.1 | convolution fusion | flops 1090256896 | bytes 2695168 | tf_op jit(solution)/shard_map/while/body/eval_jaxpr/dot_general | solution.py:51
  109.7 0.7 multiply_reduce_fusion.8
  110.9 0.6 bitcast_dynamic-update-slice_fusion.2
  112.1 7.2 %multiply_reduce_fusion.7 = f32[2048,256]{0,1:T(8,128)S(1)} fusion(f32[2048,8]{0,1:T(8,128)S(1)} %bitcast_convert_fusion.2, bf16[128,2048]{1,0:T(8,128)(2,1)} %get-tuple-element.256, s32[2048]{0:T(1024)S(1)} %bitcast.93), kind=kOutput, calls=%fused_computation.3.clone.1 | convolution fusion | flops 1090256896 | bytes 2695168 | tf_op jit(solution)/shard_map/while/body/eval_jaxpr/dot_general | solution.py:51
  119.7 0.7 multiply_reduce_fusion.8
  120.9 0.6 bitcast_dynamic-update-slice_fusion.2
  122.1 7.2 %multiply_reduce_fusion.7 = f32[2048,256]{0,1:T(8,128)S(1)} fusion(f32[2048,8]{0,1:T(8,128)S(1)} %bitcast_convert_fusion.2, bf16[128,2048]{1,0:T(8,128)(2,1)} %get-tuple-element.256, s32[2048]{0:T(1024)S(1)} %bitcast.93), kind=kOutput, calls=%fused_computation.3.clone.1 | convolution fusion | flops 1090256896 | bytes 2695168 | tf_op jit(solution)/shard_map/while/body/eval_jaxpr/dot_general | solution.py:51
  129.6 0.7 multiply_reduce_fusion.8
  130.8 0.6 bitcast_dynamic-update-slice_fusion.2
  132.0 7.2 %multiply_reduce_fusion.7 = f32[2048,256]{0,1:T(8,128)S(1)} fusion(f32[2048,8]{0,1:T(8,128)S(1)} %bitcast_convert_fusion.2, bf16[128,2048]{1,0:T(8,128)(2,1)} %get-tuple-element.256, s32[2048]{0:T(1024)S(1)} %bitcast.93), kind=kOutput, calls=%fused_computation.3.clone.1 | convolution fusion | flops 1090256896 | bytes 2695168 | tf_op jit(solution)/shard_map/while/body/eval_jaxpr/dot_general | solution.py:51
  139.6 0.7 multiply_reduce_fusion.8
  140.8 0.6 bitcast_dynamic-update-slice_fusion.2
  141.9 7.2 %multiply_reduce_fusion.7 = f32[2048,256]{0,1:T(8,128)S(1)} fusion(f32[2048,8]{0,1:T(8,128)S(1)} %bitcast_convert_fusion.2, bf16[128,2048]{1,0:T(8,128)(2,1)} %get-tuple-element.256, s32[2048]{0:T(1024)S(1)} %bitcast.93), kind=kOutput, calls=%fused_computation.3.clone.1 | convolution fusion | flops 1090256896 | bytes 2695168 | tf_op jit(solution)/shard_map/while/body/eval_jaxpr/dot_general | solution.py:51
  149.5 0.7 multiply_reduce_fusion.8
  150.7 0.6 bitcast_dynamic-update-slice_fusion.2
  151.9 7.2 %multiply_reduce_fusion.7 = f32[2048,256]{0,1:T(8,128)S(1)} fusion(f32[2048,8]{0,1:T(8,128)S(1)} %bitcast_convert_fusion.2, bf16[128,2048]{1,0:T(8,128)(2,1)} %get-tuple-element.256, s32[2048]{0:T(1024)S(1)} %bitcast.93), kind=kOutput, calls=%fused_computation.3.clone.1 | convolution fusion | flops 1090256896 | bytes 2695168 | tf_op jit(solution)/shard_map/while/body/eval_jaxpr/dot_general | solution.py:51
  159.4 0.7 multiply_reduce_fusion.8
  160.6 0.6 bitcast_dynamic-update-slice_fusion.2
  161.8 7.2 %multiply_reduce_fusion.7 = f32[2048,256]{0,1:T(8,128)S(1)} fusion(f32[2048,8]{0,1:T(8,128)S(1)} %bitcast_convert_fusion.2, bf16[128,2048]{1,0:T(8,128)(2,1)} %get-tuple-element.256, s32[2048]{0:T(1024)S(1)} %bitcast.93), kind=kOutput, calls=%fused_computation.3.clone.1 | convolution fusion | flops 1090256896 | bytes 2695168 | tf_op jit(solution)/shard_map/while/body/eval_jaxpr/dot_general | solution.py:51
  169.4 0.7 multiply_reduce_fusion.8
  170.6 0.6 bitcast_dynamic-update-slice_fusion.2
  171.7 7.2 %multiply_reduce_fusion.7 = f32[2048,256]{0,1:T(8,128)S(1)} fusion(f32[2048,8]{0,1:T(8,128)S(1)} %bitcast_convert_fusion.2, bf16[128,2048]{1,0:T(8,128)(2,1)} %get-tuple-element.256, s32[2048]{0:T(1024)S(1)} %bitcast.93), kind=kOutput, calls=%fused_computation.3.clone.1 | convolution fusion | flops 1090256896 | bytes 2695168 | tf_op jit(solution)/shard_map/while/body/eval_jaxpr/dot_general | solution.py:51
  179.3 0.7 multiply_reduce_fusion.8
  180.5 0.6 bitcast_dynamic-update-slice_fusion.2
  181.1 2.6 all-to-all-start.1
  183.8 12.0 %all-to-all-done.1 = f32[4,32,640]{2,0,1:T(4,128)S(1)} async-done(((f32[4,32,640]{2,0,1:T(4,128)}), f32[4,32,640]{2,0,1:T(4,128)S(1)}, u32[]{:S(2)}, u32[]{:S(2)}) %all-to-all-start.1) | async-done | bytes 327712 | tf_op jit(solution)/shard_map/all_to_all | solution.py:92
  195.8 5.5 %copy.38 = f32[4,32,640]{0,2,1:T(8,128)} copy(f32[4,32,640]{2,0,1:T(4,128)S(1)} %all-to-all-done.1) | data formatting | bytes 655360 | tf_op jit(solution)/shard_map/all_to_all | solution.py:92
  201.2 58.7 %gather_fusion = f32[16384,4]{1,0:T(8,128)} fusion(f32[4,20480]{0,1:T(8,128)} %bitcast.81, s32[16384]{0:T(1024)S(1)} %broadcast_clamp_fusion), kind=kCustom, calls=%fused_computation | custom fusion | bytes 589824 | tf_op jit(solution)/shard_map/gather | solution.py:93
  259.9 5.9 %copy.39 = f32[4,16384]{1,0:T(4,128)} copy(f32[4,16384]{0,1:T(8,128)} %bitcast.82) | data formatting | bytes 524288 | tf_op jit(solution)/shard_map/gather | solution.py:93
  (210 shorter events, 14.2 us)
Async XLA Ops:
  0.0 4.8 %copy-start = (s32[16384,1]{0,1:T(1,128)S(1)}, s32[16384,1]{0,1:T(1,128)}, u32[]{:S(2)}) copy-start(s32[16384,1]{0,1:T(1,128)} %param.11) | copy-start | bytes 196612
  0.0 5.0 %copy-start.2 = (s32[16384]{0:T(1024)S(1)}, s32[16384]{0:T(1024)}, u32[]{:S(2)}) copy-start(s32[16384]{0:T(1024)} %param.12) | copy-start | bytes 196612
  0.0 5.0 %copy-start.1 = (f32[3,16384]{1,0:T(4,128)S(1)}, f32[3,16384]{1,0:T(4,128)}, u32[]{:S(2)}) copy-start(f32[3,16384]{1,0:T(4,128)} %param.10) | copy-start | bytes 589828
  55.6 26.2 %copy-start.3 = (f32[8]{0:T(128)S(1)}, f32[8]{0:T(128)}, u32[]{:S(2)}) copy-start(f32[8]{0:T(128)} %constant.81) | copy-start | bytes 100
  62.2 19.4 %all-to-all-start = ((f32[4,32,640]{2,0,1:T(4,128)}), f32[4,32,640]{2,0,1:T(4,128)S(1)}, u32[]{:S(2)}, u32[]{:S(2)}) async-start(f32[4,32,640]{2,0,1:T(4,128)} %copy.33), calls=%async_computation | async-start | bytes 655360 | tf_op jit(solution)/shard_map/all_to_all | solution.py:82
  181.1 14.6 %all-to-all-start.1 = ((f32[4,32,640]{2,0,1:T(4,128)}), f32[4,32,640]{2,0,1:T(4,128)S(1)}, u32[]{:S(2)}, u32[]{:S(2)}) async-start(f32[4,32,640]{2,0,1:T(4,128)} %bitcast.14), calls=%async_computation.1 | async-start | bytes 655360 | tf_op jit(solution)/shard_map/all_to_all | solution.py:92
where the time goes:
time: 267 us; the launch traced here: 266 us
  local copies, waits for them, and re-layouts  138 us (52%)
  matrix products  72.3 us (27%)
  waiting for transfers between devices  23.8 us (9%)
  other arithmetic  20.2 us (8%)
  starting transfers between devices  10.1 us (4%)
    dot_general x10, matrix products, one_block(): jnp.dot(picker, fields, preferred_element_type=jnp.float32)  71.5 us
    gather x2, local copies, waits for them, and re-layouts, local(): return returned.reshape(4, devices * capacity)[:, flat]  64.6 us
    scatter x1, local copies, waits for them, and re-layouts, local(): jnp.zeros((4, devices * capacity), jnp.float32).at[:, flat].set(payload)  45.3 us
    all_to_all x1, waiting for transfers between devices, local(): lax.all_to_all(values, ('gx', 'gy', 'gz'), split_axis=1, concat_axis=1, t...  12 us
    all_to_all x1, waiting for transfers between devices, local(): lax.all_to_all(send.reshape(4, devices, capacity), ('gx', 'gy', 'gz'), sp...  11.8 us
    all_to_all x1, starting transfers between devices, local(): lax.all_to_all(send.reshape(4, devices, capacity), ('gx', 'gy', 'gz'), sp...  7.51 us
    dot_general x10, other arithmetic, one_block(): jnp.einsum('nfij,jn->nfi', along_t, weight_s, precision=lax.Precision.HIG...  6.96 us
    reshape x1, local copies, waits for them, and re-layouts, local(): send.reshape(4, devices, capacity)  6.68 us
  transfers between devices with their start and end apart: 2, of which 2 were waited for; matrix products, arithmetic and copies ran while one was open for 0% of the time, Pallas kernels for 0%

commit v1 on v0

v1 whole, which is shorter than its diff:
```python
import functools

import jax
import jax.numpy as jnp
import numpy as np
from jax import lax
from jax.experimental import pallas as pl
from jax.experimental.pallas import tpu as pltpu
from jax.sharding import PartitionSpec as P

AXES = ("gx", "gy", "gz")
F32, BF16 = jnp.float32, jnp.bfloat16
LANES = 128
CHUNK = 256
ROWS_PER_DOT = 4

gll_points = np.array(
    [
        -1.0,
        -0.8717401485096066,
        -0.5917001814331423,
        -0.2092992179024789,
        0.2092992179024789,
        0.5917001814331423,
        0.8717401485096066,
        1.0,
    ]
)
gll_scale = np.array(
    [1.0 / np.prod([gll_points[a] - gll_points[b] for b in range(8) if b != a]) for a in range(8)]
)
node_table = np.stack(
    [gll_scale] + [np.roll(gll_points, -k) for k in range(1, 8)], axis=0
).reshape(64, 1)


def iota_bf16(shape):
    return lax.broadcasted_iota(jnp.int32, shape, 0).astype(F32).astype(BF16)


def spread(row, count):
    return jnp.broadcast_to(row, (count, row.shape[1])).astype(BF16)


def route_kernel(count, blocks, rank_ref, coords_ref, slot_ref, prefix_ref, send_ref, row_ref, lane_ref, acc_ref):
    probes = rank_ref.shape[1]
    group = max(1, CHUNK // count)
    targets = lax.broadcasted_iota(jnp.int32, (count, CHUNK), 0)

    def place(step, carry):
        masks, hots, ranks = [], [], []
        for g in range(group):
            at = pl.ds(pl.multiple_of((step * group + g) * CHUNK, CHUNK), CHUNK)
            rank = rank_ref[:, at]
            mask = targets == jnp.broadcast_to(rank, (count, CHUNK))
            masks.append(mask)
            hots.append(jnp.where(mask, 1.0, 0.0).astype(BF16))
            ranks.append(rank.astype(F32))
        counted = jnp.dot(jnp.concatenate(hots, axis=0), prefix_ref[...], preferred_element_type=F32)
        for g in range(group):
            at = pl.ds(pl.multiple_of((step * group + g) * CHUNK, CHUNK), CHUNK)
            piece = counted[g * count : (g + 1) * count]
            place_in = jnp.where(masks[g], piece[:, :CHUNK] + carry, 0.0)
            position = jnp.sum(place_in, axis=0, keepdims=True) - 1.0
            block = jnp.floor(position * (1.0 / LANES))
            lane_ref[:, at] = position - block * LANES
            row_ref[:, at] = block * count + ranks[g]
            carry = carry + piece[:, CHUNK:]
        return carry

    lax.fori_loop(0, probes // (CHUNK * group), place, jnp.zeros((count, CHUNK), F32))

    rows = count * blocks
    row_ids = iota_bf16((rows, CHUNK))
    lane_ids = iota_bf16((LANES, CHUNK))
    acc_ref[...] = jnp.zeros_like(acc_ref)

    def scatter(step, _):
        row_hots, lane_parts = [], []
        for g in range(4):
            at = pl.ds(pl.multiple_of((step * 4 + g) * CHUNK, CHUNK), CHUNK)
            row_hots.append(
                jnp.where(row_ids == spread(row_ref[:, at], rows), jnp.ones((), BF16), jnp.zeros((), BF16))
            )
            here = lane_ids == spread(lane_ref[:, at], LANES)
            parts = []
            for v in range(3):
                value = coords_ref[v : v + 1, at]
                high = value.astype(BF16).astype(F32)
                parts += [high, value - high]
            parts.append(slot_ref[:, at].astype(F32))
            lane_parts.append(
                jnp.concatenate(
                    [jnp.where(here, spread(part, LANES), jnp.zeros((), BF16)) for part in parts], axis=0
                )
            )
        acc_ref[...] += lax.dot_general(
            jnp.concatenate(row_hots, axis=1),
            jnp.concatenate(lane_parts, axis=1),
            (((1,), (1,)), ((), ())),
            preferred_element_type=F32,
        )
        return 0

    lax.fori_loop(0, probes // (4 * CHUNK), scatter, 0)
    for b in range(blocks):
        at = slice(b * count, (b + 1) * count)
        for v in range(3):
            high = acc_ref[at, 2 * v * LANES : (2 * v + 1) * LANES]
            low = acc_ref[at, (2 * v + 1) * LANES : (2 * v + 2) * LANES]
            send_ref[v * blocks + b] = high + low
        send_ref[3 * blocks + b] = acc_ref[at, 6 * LANES : 7 * LANES]


def exchange_kernel(sizes, send_ref, recv_ref, send_sem, recv_sem, own_sem):
    count = sizes[0] * sizes[1] * sizes[2]
    me = (lax.axis_index("gx") * sizes[1] + lax.axis_index("gy")) * sizes[2] + lax.axis_index("gz")

    def coordinates_of(device):
        return (device // (sizes[1] * sizes[2]), (device // sizes[2]) % sizes[1], device % sizes[2])

    barrier = pltpu.get_barrier_semaphore()

    def greet(step, _):
        other = lax.rem(me + step, count)
        pl.semaphore_signal(
            barrier, inc=1, device_id=coordinates_of(other), device_id_type=pl.DeviceIdType.MESH
        )
        return 0

    lax.fori_loop(1, count, greet, 0)
    own = pltpu.make_async_copy(send_ref.at[:, me], recv_ref.at[:, me], own_sem)
    own.start()
    pl.semaphore_wait(barrier, count - 1)

    def copy_to(step):
        other = lax.rem(me + step, count)
        return pltpu.make_async_remote_copy(
            src_ref=send_ref.at[:, other],
            dst_ref=recv_ref.at[:, me],
            send_sem=send_sem.at[step],
            recv_sem=recv_sem.at[step],
            device_id=coordinates_of(other),
            device_id_type=pl.DeviceIdType.MESH,
        )

    def begin(step, _):
        copy_to(step).start()
        return 0

    lax.fori_loop(1, count, begin, 0)

    def finish(step, _):
        copy_to(step).wait()
        return 0

    lax.fori_loop(1, count, finish, 0)
    own.wait()


def lagrange(coord, nodes_ref):
    weight = nodes_ref[0:8, :]
    spread_coord = jnp.broadcast_to(coord, (8, LANES))
    for k in range(1, 8):
        weight = weight * (spread_coord - nodes_ref[8 * k : 8 * k + 8, :])
    return weight


def interpolate_kernel(blocks, recv_ref, fields_ref, nodes_ref, values_ref, picker_ref):
    count = recv_ref.shape[1]
    depth = fields_ref.shape[1]
    elements = depth // 8
    per_block = count // ROWS_PER_DOT
    zero = jnp.zeros((), BF16)
    ids = iota_bf16((16, LANES))

    def half(step, buffer):
        block = step // per_block
        first = (step % per_block) * ROWS_PER_DOT
        weights = []
        for j in range(ROWS_PER_DOT):
            r, s, t, slot = [recv_ref[v * blocks + block, pl.ds(first + j, 1), :] for v in range(4)]
            weights.append((lagrange(r, nodes_ref), lagrange(s, nodes_ref)))
            weight_t = lagrange(t, nodes_ref)
            columns = slice(j * LANES, (j + 1) * LANES)
            masks = [ids == spread(slot - float(16 * k), 16) for k in range(elements // 16)]
            for c in range(8):
                weight = spread(weight_t[c : c + 1, :], 16)
                for k in range(elements // 16):
                    at = c * elements + k * 16
                    picker_ref[buffer, at : at + 16, columns] = jnp.where(masks[k], weight, zero)
        along = jnp.dot(fields_ref[...], picker_ref[buffer], preferred_element_type=F32)
        for j in range(ROWS_PER_DOT):
            weight_r, weight_s = weights[j]
            columns = slice(j * LANES, (j + 1) * LANES)
            factors = [jnp.broadcast_to(weight_r[a : a + 1, :], (8, LANES)) for a in range(8)]
            for f in range(4):
                total = along[f * 64 : f * 64 + 8, columns] * factors[0]
                for a in range(1, 8):
                    total += along[f * 64 + a * 8 : f * 64 + a * 8 + 8, columns] * factors[a]
                values_ref[f * blocks + block, pl.ds(first + j, 1), :] = jnp.sum(
                    total * weight_s, axis=0, keepdims=True
                )

    def body(step, _):
        half(step * 2, 0)
        half(step * 2 + 1, 1)
        return 0

    lax.fori_loop(0, blocks * per_block // 2, body, 0)


def return_kernel(blocks, values_ref, row_ref, lane_ref, out_ref, table_ref):
    probes = row_ref.shape[1]
    count = values_ref.shape[1]
    rows = blocks * count
    for f in range(4):
        table = jnp.concatenate([values_ref[f * blocks + b] for b in range(blocks)], axis=0)
        table_ref[f * LANES : (f + 1) * LANES, :] = table.T.astype(BF16)
    row_ids = iota_bf16((rows, CHUNK))
    lane_ids = lax.broadcasted_iota(jnp.int32, (LANES, CHUNK), 0).astype(F32)

    def body(step, _):
        for g in range(2):
            at = pl.ds(pl.multiple_of((step * 2 + g) * CHUNK, CHUNK), CHUNK)
            hot = jnp.where(row_ids == spread(row_ref[:, at], rows), jnp.ones((), BF16), jnp.zeros((), BF16))
            picked = jnp.dot(table_ref[...], hot, preferred_element_type=F32)
            here = lane_ids == jnp.broadcast_to(lane_ref[:, at], (LANES, CHUNK))
            for f in range(4):
                out_ref[f : f + 1, at] = jnp.sum(
                    jnp.where(here, picked[f * LANES : (f + 1) * LANES], 0.0), axis=0, keepdims=True
                )
        return 0

    lax.fori_loop(0, probes // (2 * CHUNK), body, 0)


VMEM = pl.BlockSpec(memory_space=pltpu.VMEM)


def call(kernel, inputs, outputs, scratch, **options):
    return pl.pallas_call(
        kernel,
        out_shape=outputs,
        in_specs=[VMEM] * inputs,
        out_specs=jax.tree.map(lambda _: VMEM, outputs),
        scratch_shapes=scratch,
        compiler_params=pltpu.CompilerParams(vmem_limit_bytes=48 << 20, **options),
    )


def exchange(sizes, array, number):
    count = array.shape[1]
    return call(
        functools.partial(exchange_kernel, sizes),
        1,
        jax.ShapeDtypeStruct(array.shape, F32),
        [
            pltpu.SemaphoreType.DMA((count,)),
            pltpu.SemaphoreType.DMA((count,)),
            pltpu.SemaphoreType.DMA,
        ],
        collective_id=number,
        has_side_effects=True,
    )(array)


def local(sizes, fields, coordinates, element_rank, element_slot):
    count = sizes[0] * sizes[1] * sizes[2]
    probes = element_slot.shape[0]
    elements = fields.shape[0]
    capacity = 5 * probes // (4 * count)
    blocks = -(-capacity // LANES)
    layout = jax.ShapeDtypeStruct((4 * blocks, count, LANES), F32)
    line = jax.ShapeDtypeStruct((1, probes), F32)

    lower = np.arange(CHUNK)
    prefix = np.concatenate([lower[:, None] <= lower[None, :], np.ones((CHUNK, CHUNK))], axis=1)
    send, row, lane = call(
        functools.partial(route_kernel, count, blocks),
        4,
        (layout, line, line),
        [pltpu.VMEM((count * blocks, 7 * LANES), F32)],
    )(
        element_rank.reshape(1, probes),
        coordinates,
        element_slot.reshape(1, probes),
        jnp.asarray(prefix, BF16),
    )
    arrived = exchange(sizes, send, 0)
    turned = fields.reshape(elements, 256, 8).transpose(1, 2, 0).reshape(256, 8 * elements)
    nodes = jnp.broadcast_to(jnp.asarray(node_table, F32), (64, LANES))
    values = call(
        functools.partial(interpolate_kernel, blocks),
        3,
        layout,
        [pltpu.VMEM((2, 8 * elements, ROWS_PER_DOT * LANES), BF16)],
    )(arrived, turned, nodes)
    returned = exchange(sizes, values, 1)
    return call(
        functools.partial(return_kernel, blocks),
        3,
        jax.ShapeDtypeStruct((4, probes), F32),
        [pltpu.VMEM((4 * LANES, count * blocks), BF16)],
    )(returned, row, lane)


def solution(mesh):
    sizes = tuple(mesh.shape[axis] for axis in AXES)
    placed = (P(AXES, None), P(None, AXES), P(AXES, None), P(AXES))
    return jax.shard_map(
        functools.partial(local, sizes),
        mesh=mesh,
        in_specs=placed,
        out_specs=P(None, AXES),
        check_vma=False,
    )
```

time: 267 us -> 75.1 us (0.28)
  local copies, waits for them, and re-layouts: 138 us -> 4.67 us
  matrix products: 72.3 us -> 0 us
  Pallas kernels: 0 us -> 70.1 us
  waiting for transfers between devices: 23.8 us -> 0 us
  other arithmetic: 20.2 us -> 0 us
  starting transfers between devices: 10.1 us -> 0 us
    dot_general x11 -> x0, matrix products: 72.3 us -> none  [the longest x10 71.5 us: one_block(): jnp.dot(picker, fields, preferred_element_type=jnp.float32)]
    pallas_call x0 -> x5, Pallas kernels: none -> 70.1 us  [the longest x2 29.2 us: exchange(): call(functools.partial(exchange_kernel, sizes), 1, jax.ShapeDtypeStruct(a...]
    gather x2 -> x0, local copies, waits for them, and re-layouts: 64.6 us -> none  [local(): return returned.reshape(4, devices * capacity)[:, flat]]
    scatter x1 -> x0, local copies, waits for them, and re-layouts: 45.3 us -> none  [local(): jnp.zeros((4, devices * capacity), jnp.float32).at[:, flat].set(payload)]
    all_to_all x2 -> x0, waiting for transfers between devices: 23.8 us -> none  [the longest x1 12 us: local(): lax.all_to_all(values, ('gx', 'gy', 'gz'), split_axis=1, concat_axis=1, t...]
    all_to_all x2 -> x0, starting transfers between devices: 10.1 us -> none  [the longest x1 7.51 us: local(): lax.all_to_all(send.reshape(4, devices, capacity), ('gx', 'gy', 'gz'), sp...]
    dot_general x20 -> x0, other arithmetic: 7.86 us -> none  [the longest x10 6.96 us: one_block(): jnp.einsum('nfij,jn->nfi', along_t, weight_s, precision=lax.Precision.HIG...]
    reshape x1 -> x0, local copies, waits for them, and re-layouts: 6.68 us -> none  [local(): send.reshape(4, devices, capacity)]
  transfers between devices with their start and end apart: 2 -> 0, of which waited for: 2 -> 0; matrix products, arithmetic and copies ran while one was open for 0% -> 0% of each run, Pallas kernels for 0% -> 0%
where the time goes in v1:
time: 75.1 us; the launch traced here: 74.9 us
  Pallas kernels  70.1 us (93%)
  local copies, waits for them, and re-layouts  4.67 us (6%)
    pallas_call x2, Pallas kernels, exchange(): call(functools.partial(exchange_kernel, sizes), 1, jax.ShapeDtypeStruct(a...  29.2 us
    pallas_call x1, Pallas kernels, local(): call(functools.partial(interpolate_kernel, blocks), 3, layout, [pltpu.VME...  16.2 us
    pallas_call x1, Pallas kernels, local(): call(functools.partial(route_kernel, count, blocks), 4, (layout, line, li...  14.3 us
    pallas_call x1, Pallas kernels, local(): call(functools.partial(return_kernel, blocks), 3, jax.ShapeDtypeStruct((4...  10.4 us
    unnamed x14, local copies, waits for them, and re-layouts  4.6 us

profile of v1, /device:TPU:0, one launch (start us, length us, event | category | flops | bytes accessed | tf_op | source)
XLA Modules:
  0.0 74.9 jit_solution(7321123890142966885)
XLA Ops:
  0.0 0.0 copy-start
  0.0 0.9 %copy-done = f32[3,16384]{1,0:T(4,128)S(1)} copy-done((f32[3,16384]{1,0:T(4,128)S(1)}, f32[3,16384]{1,0:T(4,128)}, u32[]{:S(2)}) %copy-start) | copy-done | bytes 196632
  1.0 0.0 copy-start.1
  1.0 0.9 %copy-done.1 = bf16[256,512]{1,0:T(8,128)(2,1)S(1)} copy-done((bf16[256,512]{1,0:T(8,128)(2,1)S(1)}, bf16[256,512]{1,0:T(8,128)(2,1)}, u32[]{:S(2)}) %copy-start.1) | copy-done | bytes 262168
  1.9 0.0 copy-start.2
  1.9 0.8 %copy-done.2 = s32[16384,1]{0,1:T(1,128)S(1)} copy-done((s32[16384,1]{0,1:T(1,128)S(1)}, s32[16384,1]{0,1:T(1,128)}, u32[]{:S(2)}) %copy-start.2) | copy-done | bytes 65560
  2.7 0.0 copy-start.3
  2.7 0.8 %copy-done.3 = s32[16384]{0:T(1024)S(1)} copy-done((s32[16384]{0:T(1024)S(1)}, s32[16384]{0:T(1024)}, u32[]{:S(2)}) %copy-start.3) | copy-done | bytes 65560
  3.6 0.0 copy-start.4
  3.6 14.3 %shard_map.64 = (f32[20,32,128]{2,1,0:T(8,128)S(1)}, f32[1,16384]{1,0:T(1,128)S(1)}, f32[1,16384]{1,0:T(1,128)S(1)}) custom-call(s32[1,16384]{1,0:T(1,128)S(1)} %bitcast.10, f32[3,16384]{1,0:T(4,128)S(1)} %copy-done, s32[1,16384]{1,0:T(1,128)S(1)} %bitcast.11, bf16[256,512]{1,0:T(8,128)(2,1)S(1)} %copy-done.1), custom_call_target="tpu_custom_call" | custom-call | tf_op jit(solution)/shard_map/pallas_call | solution.py:279
  17.9 15.8 %shard_map.65.recv_ref = f32[20,32,128]{2,1,0:T(8,128)S(1)} custom-call(f32[20,32,128]{2,1,0:T(8,128)S(1)} %get-tuple-element.8.send_ref), custom_call_target="tpu_custom_call" | custom-call | tf_op jit(solution)/shard_map/pallas_call | solution.py:254
  33.8 0.0 copy-done.4
  33.8 0.3 copy.8
  34.0 0.1 copy.11
  34.1 0.0 copy-start.5
  34.2 0.6 copy-done.5
  34.8 0.1 broadcast_in_dim.8.nodes_ref
  34.9 16.2 %shard_map.66.send_ref = f32[20,32,128]{2,1,0:T(8,128)S(1)} custom-call(f32[20,32,128]{2,1,0:T(8,128)S(1)} %shard_map.65.recv_ref, bf16[256,1024]{1,0:T(8,128)(2,1)S(1)} %bitcast.9, f32[64,128]{1,0:T(8,128)S(1)} %broadcast_in_dim.8.nodes_ref), custom_call_target="tpu_custom_call" | custom-call | tf_op jit(solution)/shard_map/pallas_call | solution.py:293
  51.1 13.4 %shard_map.67.values_ref = f32[20,32,128]{2,1,0:T(8,128)S(1)} custom-call(f32[20,32,128]{2,1,0:T(8,128)S(1)} %shard_map.66.send_ref), custom_call_target="tpu_custom_call" | custom-call | tf_op jit(solution)/shard_map/pallas_call | solution.py:254
  64.5 10.4 %shard_map.68 = f32[4,16384]{1,0:T(4,128)} custom-call(f32[20,32,128]{2,1,0:T(8,128)S(1)} %shard_map.67.values_ref, f32[1,16384]{1,0:T(1,128)S(1)} %get-tuple-element.9.row_ref, f32[1,16384]{1,0:T(1,128)S(1)} %get-tuple-element.10.lane_ref), custom_call_target="tpu_custom_call" | custom-call | tf_op jit(solution)/shard_map/pallas_call | solution.py:300
Async XLA Ops:
  0.0 0.9 %copy-start = (f32[3,16384]{1,0:T(4,128)S(1)}, f32[3,16384]{1,0:T(4,128)}, u32[]{:S(2)}) copy-start(f32[3,16384]{1,0:T(4,128)} %coords_ref.1) | copy-start | bytes 589828
  1.0 0.9 %copy-start.1 = (bf16[256,512]{1,0:T(8,128)(2,1)S(1)}, bf16[256,512]{1,0:T(8,128)(2,1)}, u32[]{:S(2)}) copy-start(bf16[256,512]{1,0:T(8,128)(2,1)} %constant.4.clone.prefix_ref) | copy-start | bytes 786436
  1.9 0.8 %copy-start.2 = (s32[16384,1]{0,1:T(1,128)S(1)}, s32[16384,1]{0,1:T(1,128)}, u32[]{:S(2)}) copy-start(s32[16384,1]{0,1:T(1,128)} %param.8) | copy-start | bytes 196612
  2.7 0.8 %copy-start.3 = (s32[16384]{0:T(1024)S(1)}, s32[16384]{0:T(1024)}, u32[]{:S(2)}) copy-start(s32[16384]{0:T(1024)} %param.9) | copy-start | bytes 196612
  3.6 30.2 %copy-start.4 = (bf16[128,2048]{1,0:T(8,128)(2,1)S(1)}, bf16[128,2048]{1,0:T(8,128)(2,1)}, u32[]{:S(2)}) copy-start(bf16[128,2048]{1,0:T(8,128)(2,1)} %param.6) | copy-start | bytes 1572868
  34.1 0.7 copy-start.5

commit v2 on v1

v2 whole, which is shorter than its diff:
```python
import functools

import jax
import jax.numpy as jnp
import numpy as np
from jax import lax
from jax.experimental import pallas as pl
from jax.experimental.pallas import tpu as pltpu
from jax.sharding import PartitionSpec as P

AXES = ("gx", "gy", "gz")
F32, BF16 = jnp.float32, jnp.bfloat16
LANES = 128
CHUNK = 256
GROUP = 4

gll_points = np.array(
    [
        -1.0,
        -0.8717401485096066,
        -0.5917001814331423,
        -0.2092992179024789,
        0.2092992179024789,
        0.5917001814331423,
        0.8717401485096066,
        1.0,
    ]
)
gll_scale = np.array(
    [1.0 / np.prod([gll_points[a] - gll_points[b] for b in range(8) if b != a]) for a in range(8)]
)
node_table = np.stack(
    [gll_scale] + [np.roll(gll_points, -k) for k in range(1, 8)], axis=0
).reshape(64, 1)


def iota_bf16(shape):
    return lax.broadcasted_iota(jnp.int32, shape, 0).astype(F32).astype(BF16)


def spread(row, count):
    return jnp.broadcast_to(row, (count, row.shape[1])).astype(BF16)


def route(count, blocks, rank_ref, coords_ref, slot_ref, prefix_ref, send_ref, row_ref, lane_ref, acc_ref):
    probes = rank_ref.shape[1]
    group = max(1, CHUNK // count)
    targets = lax.broadcasted_iota(jnp.int32, (count, CHUNK), 0)

    def place(step, carry):
        masks, hots, ranks = [], [], []
        for g in range(group):
            at = pl.ds(pl.multiple_of((step * group + g) * CHUNK, CHUNK), CHUNK)
            rank = rank_ref[:, at]
            mask = targets == jnp.broadcast_to(rank, (count, CHUNK))
            masks.append(mask)
            hots.append(jnp.where(mask, 1.0, 0.0).astype(BF16))
            ranks.append(rank.astype(F32))
        counted = jnp.dot(jnp.concatenate(hots, axis=0), prefix_ref[...], preferred_element_type=F32)
        for g in range(group):
            at = pl.ds(pl.multiple_of((step * group + g) * CHUNK, CHUNK), CHUNK)
            piece = counted[g * count : (g + 1) * count]
            place_in = jnp.where(masks[g], piece[:, :CHUNK] + carry, 0.0)
            position = jnp.sum(place_in, axis=0, keepdims=True) - 1.0
            block = jnp.floor(position * (1.0 / LANES))
            lane_ref[:, at] = position - block * LANES
            row_ref[:, at] = block * count + ranks[g]
            carry = carry + piece[:, CHUNK:]
        return carry

    lax.fori_loop(0, probes // (CHUNK * group), place, jnp.zeros((count, CHUNK), F32))

    rows = count * blocks
    part_lanes = LANES // 2
    row_ids = iota_bf16((rows, CHUNK))
    lane_ids = iota_bf16((part_lanes, CHUNK))
    one, zero = jnp.ones((), BF16), jnp.zeros((), BF16)
    acc_ref[...] = jnp.zeros_like(acc_ref)

    def scatter(step, _):
        row_hots, lane_parts = [], []
        for g in range(4):
            at = pl.ds(pl.multiple_of((step * 4 + g) * CHUNK, CHUNK), CHUNK)
            row, lane = row_ref[:, at], lane_ref[:, at]
            upper = lane >= float(part_lanes)
            halves = [jnp.where(upper, -1.0, row), jnp.where(upper, row, -1.0)]
            row_hots.append(
                jnp.concatenate([jnp.where(row_ids == spread(part, rows), one, zero) for part in halves], axis=0)
            )
            here = lane_ids == spread(jnp.where(upper, lane - float(part_lanes), lane), part_lanes)
            parts = []
            for v in range(3):
                value = coords_ref[v : v + 1, at]
                high = value.astype(BF16).astype(F32)
                parts += [high, value - high]
            parts.append(slot_ref[:, at].astype(F32))
            chosen = [jnp.where(here, spread(part, part_lanes), zero) for part in parts]
            chosen.append(jnp.zeros((part_lanes, CHUNK), BF16))
            lane_parts.append(jnp.concatenate(chosen, axis=0))
        acc_ref[...] += lax.dot_general(
            jnp.concatenate(row_hots, axis=1),
            jnp.concatenate(lane_parts, axis=1),
            (((1,), (1,)), ((), ())),
            preferred_element_type=F32,
        )
        return 0

    lax.fori_loop(0, probes // (4 * CHUNK), scatter, 0)
    left = lax.broadcasted_iota(jnp.int32, (count, LANES), 1) < part_lanes
    for b in range(blocks):
        for v in range(4):
            sides = []
            for h in range(2):
                first = h * rows + b * count
                both = acc_ref[first : first + count, v * LANES : (v + 1) * LANES]
                sides.append(both + pltpu.roll(both, part_lanes, 1))
            send_ref[v * blocks + b] = jnp.where(left, sides[0], sides[1])


def lagrange(coord, nodes_ref):
    weight = nodes_ref[0:8, :]
    spread_coord = jnp.broadcast_to(coord, (8, LANES))
    for k in range(1, 8):
        weight = weight * (spread_coord - nodes_ref[8 * k : 8 * k + 8, :])
    return weight


def interpolate(blocks, block, sources, recv_ref, fields_ref, nodes_ref, values_ref, picker_ref):
    depth = fields_ref.shape[1]
    elements = depth // 8
    zero = jnp.zeros((), BF16)
    ids = iota_bf16((16, LANES))
    weights = []
    for j, source in enumerate(sources):
        r, s, t, slot = [recv_ref[v * blocks + block, pl.ds(source, 1), :] for v in range(4)]
        weights.append((lagrange(r, nodes_ref), lagrange(s, nodes_ref)))
        weight_t = lagrange(t, nodes_ref)
        columns = slice(j * LANES, (j + 1) * LANES)
        masks = [ids == spread(slot - float(16 * k), 16) for k in range(elements // 16)]
        for c in range(8):
            weight = spread(weight_t[c : c + 1, :], 16)
            for k in range(elements // 16):
                at = c * elements + k * 16
                picker_ref[at : at + 16, columns] = jnp.where(masks[k], weight, zero)
    along = jnp.dot(fields_ref[...], picker_ref[...], preferred_element_type=F32)
    for j, source in enumerate(sources):
        weight_r, weight_s = weights[j]
        columns = slice(j * LANES, (j + 1) * LANES)
        factors = [jnp.broadcast_to(weight_r[a : a + 1, :], (8, LANES)) for a in range(8)]
        for f in range(4):
            total = along[f * 64 : f * 64 + 8, columns] * factors[0]
            for a in range(1, 8):
                total += along[f * 64 + a * 8 : f * 64 + a * 8 + 8, columns] * factors[a]
            values_ref[f * blocks + block, pl.ds(source, 1), :] = jnp.sum(
                total * weight_s, axis=0, keepdims=True
            )


def sample_kernel(
    sizes,
    blocks,
    rank_ref,
    coords_ref,
    slot_ref,
    prefix_ref,
    fields_ref,
    nodes_ref,
    back_ref,
    row_ref,
    lane_ref,
    acc_ref,
    send_ref,
    recv_ref,
    values_ref,
    picker_even,
    picker_odd,
    out_sem,
    in_sem,
    back_out_sem,
    back_in_sem,
    own_sem,
):
    count = sizes[0] * sizes[1] * sizes[2]
    me = (lax.axis_index("gx") * sizes[1] + lax.axis_index("gy")) * sizes[2] + lax.axis_index("gz")
    mesh_ids = pl.DeviceIdType.MESH

    def coordinates_of(device):
        return (device // (sizes[1] * sizes[2]), (device // sizes[2]) % sizes[1], device % sizes[2])

    def each(first, last, act):
        def body(step, _):
            act(step)
            return 0

        lax.fori_loop(first, last, body, 0)

    def behind(step):
        return lax.rem(me + count - step, count)

    def outward(step):
        other = lax.rem(me + step, count)
        return pltpu.make_async_remote_copy(
            src_ref=send_ref.at[:, other],
            dst_ref=recv_ref.at[:, me],
            send_sem=out_sem.at[step],
            recv_sem=in_sem.at[step],
            device_id=coordinates_of(other),
            device_id_type=mesh_ids,
        )

    def backward(step):
        other = behind(step)
        return pltpu.make_async_remote_copy(
            src_ref=values_ref.at[:, other],
            dst_ref=back_ref.at[:, me],
            send_sem=back_out_sem.at[step],
            recv_sem=back_in_sem.at[step],
            device_id=coordinates_of(other),
            device_id_type=mesh_ids,
        )

    barrier = pltpu.get_barrier_semaphore()
    each(
        1,
        count,
        lambda step: pl.semaphore_signal(
            barrier, inc=1, device_id=coordinates_of(lax.rem(me + step, count)), device_id_type=mesh_ids
        ),
    )
    route(count, blocks, rank_ref, coords_ref, slot_ref, prefix_ref, send_ref, row_ref, lane_ref, acc_ref)
    pl.semaphore_wait(barrier, count - 1)
    each(1, count, lambda step: outward(step).start())
    own = pltpu.make_async_copy(send_ref.at[:, me], recv_ref.at[:, me], own_sem.at[0])
    own.start()
    own.wait()
    own_back = pltpu.make_async_copy(values_ref.at[:, me], back_ref.at[:, me], own_sem.at[1])
    pickers = [picker_even, picker_odd]

    def reply(group):
        for j in range(GROUP):
            step = group * GROUP + j
            if j == 0:

                @pl.when(step == 0)
                def _():
                    own_back.start()

                @pl.when(step > 0)
                def _():
                    backward(step).start()

            else:
                backward(step).start()

    def body(group, _):
        sources = []
        for j in range(GROUP):
            step = group * GROUP + j
            if j == 0:

                @pl.when(step > 0)
                def _():
                    outward(step).wait_recv()

            else:
                outward(step).wait_recv()
            sources.append(behind(step))
        for block in range(blocks):
            interpolate(blocks, block, sources, recv_ref, fields_ref, nodes_ref, values_ref, pickers[block % 2])

        @pl.when(group > 0)
        def _():
            reply(group - 1)

        return 0

    groups = count // GROUP
    lax.fori_loop(0, groups, body, 0)
    each(1, count, lambda step: outward(step).wait_send())
    reply(groups - 1)
    each(1, count, lambda step: backward(step).wait())
    own_back.wait()


def return_kernel(blocks, values_ref, row_ref, lane_ref, out_ref, table_ref):
    probes = row_ref.shape[1]
    count = values_ref.shape[1]
    rows = blocks * count
    for f in range(4):
        table = jnp.concatenate([values_ref[f * blocks + b] for b in range(blocks)], axis=0)
        table_ref[f * LANES : (f + 1) * LANES, :] = table.T.astype(BF16)
    row_ids = iota_bf16((rows, CHUNK))
    lane_ids = lax.broadcasted_iota(jnp.int32, (LANES, CHUNK), 0).astype(F32)

    def body(step, _):
        for g in range(4):
            at = pl.ds(pl.multiple_of((step * 4 + g) * CHUNK, CHUNK), CHUNK)
            hot = jnp.where(row_ids == spread(row_ref[:, at], rows), jnp.ones((), BF16), jnp.zeros((), BF16))
            picked = jnp.dot(table_ref[...], hot, preferred_element_type=F32)
            here = lane_ids == jnp.broadcast_to(lane_ref[:, at], (LANES, CHUNK))
            for f in range(4):
                out_ref[f : f + 1, at] = jnp.sum(
                    jnp.where(here, picked[f * LANES : (f + 1) * LANES], 0.0), axis=0, keepdims=True
                )
        return 0

    lax.fori_loop(0, probes // (4 * CHUNK), body, 0)


VMEM = pl.BlockSpec(memory_space=pltpu.VMEM)


def call(kernel, inputs, outputs, scratch, **options):
    return pl.pallas_call(
        kernel,
        out_shape=outputs,
        in_specs=[VMEM] * inputs,
        out_specs=jax.tree.map(lambda _: VMEM, outputs),
        scratch_shapes=scratch,
        compiler_params=pltpu.CompilerParams(vmem_limit_bytes=48 << 20, **options),
    )


def local(sizes, fields, coordinates, element_rank, element_slot):
    count = sizes[0] * sizes[1] * sizes[2]
    probes = element_slot.shape[0]
    elements = fields.shape[0]
    capacity = 5 * probes // (4 * count)
    blocks = -(-capacity // LANES)
    layout = jax.ShapeDtypeStruct((4 * blocks, count, LANES), F32)
    line = jax.ShapeDtypeStruct((1, probes), F32)

    lower = np.arange(CHUNK)
    prefix = np.concatenate([lower[:, None] <= lower[None, :], np.ones((CHUNK, CHUNK))], axis=1)
    turned = fields.reshape(elements, 256, 8).transpose(1, 2, 0).reshape(256, 8 * elements)
    nodes = jnp.broadcast_to(jnp.asarray(node_table, F32), (64, LANES))
    picker = pltpu.VMEM((8 * elements, GROUP * LANES), BF16)
    buffer = pltpu.VMEM(layout.shape, F32)
    arrivals = pltpu.SemaphoreType.DMA((count,))
    returned, row, lane = call(
        functools.partial(sample_kernel, sizes, blocks),
        6,
        (layout, line, line),
        [pltpu.VMEM((2 * count * blocks, 4 * LANES), F32)]
        + [buffer] * 3
        + [picker] * 2
        + [arrivals] * 4
        + [pltpu.SemaphoreType.DMA((2,))],
        collective_id=0,
        has_side_effects=True,
    )(
        element_rank.reshape(1, probes),
        coordinates,
        element_slot.reshape(1, probes),
        jnp.asarray(prefix, BF16),
        turned,
        nodes,
    )
    return call(
        functools.partial(return_kernel, blocks),
        3,
        jax.ShapeDtypeStruct((4, probes), F32),
        [pltpu.VMEM((4 * LANES, count * blocks), BF16)],
    )(returned, row, lane)


def solution(mesh):
    sizes = tuple(mesh.shape[axis] for axis in AXES)
    placed = (P(AXES, None), P(None, AXES), P(AXES, None), P(AXES))
    return jax.shard_map(
        functools.partial(local, sizes),
        mesh=mesh,
        in_specs=placed,
        out_specs=P(None, AXES),
        check_vma=False,
    )
```

time: 75.1 us -> 53.9 us (0.72)
  Pallas kernels: 70.1 us -> 51.4 us
  local copies, waits for them, and re-layouts: 4.67 us -> 2.3 us
    pallas_call x4 -> x1, Pallas kernels: 59.7 us -> 43.5 us  [local(): call(functools.partial(sample_kernel, sizes, blocks), 6, (layout, line, l...]
    pallas_call x1, Pallas kernels: 10.4 us -> 7.88 us  [local(): call(functools.partial(return_kernel, blocks), 3, jax.ShapeDtypeStruct((4...]
    unnamed x14 -> x12, local copies, waits for them, and re-layouts: 4.6 us -> 2.23 us
where the time goes in v2:
time: 53.9 us; the launch traced here: 53.8 us
  Pallas kernels  51.4 us (95%)
  local copies, waits for them, and re-layouts  2.3 us (4%)
    pallas_call x1, Pallas kernels, local(): call(functools.partial(sample_kernel, sizes, blocks), 6, (layout, line, l...  43.5 us
    pallas_call x1, Pallas kernels, local(): call(functools.partial(return_kernel, blocks), 3, jax.ShapeDtypeStruct((4...  7.88 us
    unnamed x12, local copies, waits for them, and re-layouts  2.23 us

profile of v2, /device:TPU:0, one launch (start us, length us, event | category | flops | bytes accessed | tf_op | source)
XLA Modules:
  0.0 53.8 jit_solution(10963209145285928898)
XLA Ops:
  0.0 1.3 %copy.8 = bf16[128,2048]{0,1:T(8,128)(2,1)S(1)} copy(bf16[128,2048]{1,0:T(8,128)(2,1)} %param.6) | data formatting | bytes 1048576 | tf_op args[0]
  1.3 0.0 copy-start
  1.3 0.0 copy-start.1
  1.3 0.0 copy-start.2
  1.4 0.0 copy-start.3
  1.4 0.1 copy.11
  1.5 0.0 copy-start.4
  1.5 0.7 %copy-done.4 = f32[64]{0:T(128)S(1)} copy-done((f32[64]{0:T(128)S(1)}, f32[64]{0:T(128)}, u32[]{:S(2)}) %copy-start.4) | copy-done | bytes 280
  2.2 0.1 broadcast_in_dim.8.nodes_ref
  2.2 0.0 copy-done
  2.3 0.1 copy-done.1
  2.4 0.0 copy-done.2
  2.4 0.0 copy-done.3
  2.4 43.5 %shard_map.64 = (f32[20,32,128]{2,1,0:T(8,128)S(1)}, f32[1,16384]{1,0:T(1,128)S(1)}, f32[1,16384]{1,0:T(1,128)S(1)}) custom-call(s32[1,16384]{1,0:T(1,128)S(1)} %bitcast.10, f32[3,16384]{1,0:T(4,128)S(1)} %copy-done, s32[1,16384]{1,0:T(1,128)S(1)} %bitcast.11, bf16[256,512]{1,0:T(8,128)(2,1)S(1)} %copy-done.1, bf16[256,1024]{1,0:T(8,128)(2,1)S(1)} %bitcast.9, ...), custom_call_target="tpu_custom_call" | custom-call | tf_op jit(solution)/shard_map/pallas_call | solution.py:340
  45.9 7.9 %shard_map.65 = f32[4,16384]{1,0:T(4,128)} custom-call(f32[20,32,128]{2,1,0:T(8,128)S(1)} %get-tuple-element.8.values_ref, f32[1,16384]{1,0:T(1,128)S(1)} %get-tuple-element.9.row_ref, f32[1,16384]{1,0:T(1,128)S(1)} %get-tuple-element.10.lane_ref), custom_call_target="tpu_custom_call" | custom-call | tf_op jit(solution)/shard_map/pallas_call | solution.py:359
Async XLA Ops:
  1.3 1.0 %copy-start = (f32[3,16384]{1,0:T(4,128)S(1)}, f32[3,16384]{1,0:T(4,128)}, u32[]{:S(2)}) copy-start(f32[3,16384]{1,0:T(4,128)} %coords_ref.1) | copy-start | bytes 589828
  1.3 1.0 %copy-start.1 = (bf16[256,512]{1,0:T(8,128)(2,1)S(1)}, bf16[256,512]{1,0:T(8,128)(2,1)}, u32[]{:S(2)}) copy-start(bf16[256,512]{1,0:T(8,128)(2,1)} %constant.5.clone.prefix_ref) | copy-start | bytes 786436
  1.3 1.0 %copy-start.2 = (s32[16384,1]{0,1:T(1,128)S(1)}, s32[16384,1]{0,1:T(1,128)}, u32[]{:S(2)}) copy-start(s32[16384,1]{0,1:T(1,128)} %param.8) | copy-start | bytes 196612
  1.4 1.0 %copy-start.3 = (s32[16384]{0:T(1024)S(1)}, s32[16384]{0:T(1024)}, u32[]{:S(2)}) copy-start(s32[16384]{0:T(1024)} %param.9) | copy-start | bytes 196612
  1.5 0.7 %copy-start.4 = (f32[64]{0:T(128)S(1)}, f32[64]{0:T(128)}, u32[]{:S(2)}) copy-start(f32[64]{0:T(128)} %constant.6) | copy-start | bytes 772
